TPU v7x, 128 devices: a whole 4x4x4 slice. The times are simulated.
128 devices in a mesh: gx: 16 (over y, x_lo, core), gy: 8 (over z, x_hi).
Axes of the slice: x: 4 (x_hi: 2, x_lo: 2; x = x_hi * 2 + x_lo), y: 4, z: 4, core: 2. Of those that a mesh axis runs over, the one named last changes fastest.
Arguments:
- thinker_normed: bfloat16 [8, 16, 8192], P(None, None, 'gx'), may hold values from -6 to 6
- thinker_resid: bfloat16 [8, 16, 8192], P('gy', None, 'gx'), may hold values from -6 to 6
- gate_weight: bfloat16 [8192, 29568], P('gx', 'gy'), may hold values from -0.0625 to 0.0625
- up_weight: bfloat16 [8192, 29568], P('gx', 'gy'), may hold values from -0.0625 to 0.0625
- down_weight: bfloat16 [29568, 8192], P('gy', 'gx'), may hold values from -0.03125 to 0.03125
- bridge_weight: bfloat16 [8192, 3584], P('gx'), may hold values from -0.0625 to 0.0625
- talker_stream: bfloat16 [8, 3072, 3584], P('gy', 'gx'), may hold values from -6 to 6
- norm_gain: float32 [3584], replicated, may hold values from 0.5 to 2
- w_query: bfloat16 [3584, 1792], P(None, 'gy'), may hold values from -0.09375 to 0.09375
- w_key: bfloat16 [3584, 256], P(None, 'gy'), may hold values from -0.09375 to 0.09375
- w_value: bfloat16 [3584, 256], P(None, 'gy'), may hold values from -0.09375 to 0.09375
- a_query: bfloat16 [3584, 64], replicated, may hold values from -0.09375 to 0.09375
- b_query: bfloat16 [64, 1792], replicated, may hold values from -0.75 to 0.75
- a_value: bfloat16 [3584, 64], replicated, may hold values from -0.09375 to 0.09375
- b_value: bfloat16 [64, 256], replicated, may hold values from -0.75 to 0.75
- text_index: int32 [8, 3072], P('gy', 'gx'), may hold values from 0 to 15
- span_offset: int32 [8], P('gy'), may hold values from 1 to 3071
- out_grad: bfloat16 [8, 3072, 1792], P('gy', 'gx'), may hold values from -6 to 6
Outputs:
- attn_out: bfloat16 [8, 3072, 1792], P('gy', 'gx')
- grad_aq: float32 [3584, 64], replicated
- grad_bq: float32 [64, 1792], replicated
- grad_av: float32 [3584, 64], replicated
- grad_bv: float32 [64, 256], replicated
All inputs are finite; a program needn't handle non-finite values.
Results may differ from a plain program's by a relative error of at most 0.035.
Values may be sent and summed in bfloat16 or wider, within the bound.
A program may use at most 192 MiB of HBM per device.

v0:
```python
import math
import jax
import jax.numpy as jnp
from jax import lax
from jax.sharding import PartitionSpec as P

HEADS = 14
KVH = 2
HD = 128
rope_base = 1000000.0
norm_eps = 1e-06


def cut_along(array, dim, size):
    dims = array.shape
    parts = array.reshape(*dims[:dim], size, dims[dim] // size, *dims[dim + 1 :])
    return jnp.moveaxis(parts, dim, 0)


def sent_and_summed(array, axis, dim):
    size = lax.axis_size(axis)
    parts = lax.all_to_all(cut_along(array, dim, size), axis, 0, 0, tiled=True)
    return jnp.sum(parts, axis=0)


def angle_tables(first_pos, length):
    position = (first_pos + jnp.arange(length, dtype=jnp.int32)).astype(jnp.float32)
    frequency = rope_base ** (-(2.0 * jnp.arange(HD // 2, dtype=jnp.float32)) / HD)
    angles = position[:, None] * frequency[None, :]
    return (jnp.cos(angles), jnp.sin(angles))


def rotate(tensor, cosine, sine_table, signed):
    layout = (cosine.shape[0],) + (1,) * (tensor.ndim - 2) + (cosine.shape[1],)
    cosine = cosine.reshape(layout)
    sine_part = sine_table.reshape(layout) * signed
    half_width = tensor.shape[-1] // 2
    first_half = tensor[..., :half_width]
    second_half = tensor[..., half_width:]
    return jnp.concatenate(
        [
            first_half * cosine - second_half * sine_part,
            second_half * cosine + first_half * sine_part,
        ],
        axis=-1,
    )


def on_device(
    thinker_normed,
    thinker_resid,
    gate_weight,
    up_weight,
    down_weight,
    bridge_weight,
    talker_stream,
    norm_gain,
    w_query,
    w_key,
    w_value,
    a_query,
    b_query,
    a_value,
    b_value,
    text_index,
    span_offset,
    out_grad,
):
    seq_count, rows_seq, columns = thinker_normed.shape
    normed = thinker_normed.reshape(seq_count * rows_seq, columns)
    ff_local = gate_weight.shape[1]
    block = normed
    gate_part = jnp.dot(block, gate_weight, preferred_element_type=jnp.float32)
    up_part = jnp.dot(block, up_weight, preferred_element_type=jnp.float32)
    both_parts = sent_and_summed(jnp.concatenate([gate_part, up_part], axis=1), "gx", 0)
    hidden = (jax.nn.silu(both_parts[:, :ff_local]) * both_parts[:, ff_local:]).astype(jnp.bfloat16)
    partial_out = jnp.dot(
        lax.all_gather(hidden, "gx", axis=0, tiled=True),
        down_weight,
        preferred_element_type=jnp.float32,
    )
    summed = sent_and_summed(partial_out, "gy", 0)
    thinker_out = (summed + thinker_resid[0].astype(jnp.float32)).astype(jnp.bfloat16)
    bridge_part = jnp.dot(thinker_out, bridge_weight, preferred_element_type=jnp.float32)
    bridge = lax.psum(bridge_part, "gx").astype(jnp.bfloat16)
    tokens = talker_stream.shape[1]
    groups = HEADS // KVH
    scale = 1.0 / math.sqrt(HD)
    picks = (text_index[0][:, None] == jnp.arange(rows_seq, dtype=jnp.int32)[None, :]).astype(
        jnp.bfloat16
    )
    mixed = talker_stream[0].astype(jnp.float32) + jnp.dot(
        picks, bridge, preferred_element_type=jnp.float32
    )
    normal = (
        mixed * lax.rsqrt(jnp.mean(mixed * mixed, axis=1, keepdims=True) + norm_eps) * norm_gain
    ).astype(jnp.bfloat16)
    low_query = jnp.dot(normal, a_query, preferred_element_type=jnp.float32).astype(jnp.bfloat16)
    low_value = jnp.dot(normal, a_value, preferred_element_type=jnp.float32).astype(jnp.bfloat16)
    slab_rows = lax.all_gather(normal, "gy", axis=0, tiled=True)
    projected = jnp.concatenate(
        [
            jnp.dot(slab_rows, w_query, preferred_element_type=jnp.float32),
            jnp.dot(slab_rows, w_key, preferred_element_type=jnp.float32),
            jnp.dot(slab_rows, w_value, preferred_element_type=jnp.float32),
        ],
        axis=1,
    )
    returned = lax.all_to_all(projected, "gy", split_axis=0, concat_axis=1, tiled=True)
    parcels = returned.reshape(tokens, lax.axis_size("gy"), -1)
    query_cols = w_query.shape[1]
    key_cols = w_key.shape[1]
    base_query = parcels[:, :, :query_cols].reshape(tokens, -1)
    base_key = parcels[:, :, query_cols : query_cols + key_cols].reshape(tokens, -1)
    base_value = parcels[:, :, query_cols + key_cols :].reshape(tokens, -1)
    first_pos = lax.axis_index("gx") * tokens
    cosine, sine_table = angle_tables(first_pos, tokens)
    query_pre = base_query + jnp.dot(low_query, b_query, preferred_element_type=jnp.float32)
    query = rotate(query_pre.reshape(tokens, KVH, groups, HD), cosine, sine_table, 1.0).astype(
        jnp.bfloat16
    )
    key_local = (
        rotate(base_key.reshape(tokens, KVH, HD), cosine, sine_table, 1.0)
        .astype(jnp.bfloat16)
        .reshape(tokens, KVH * HD)
    )
    value_local = (
        base_value + jnp.dot(low_value, b_value, preferred_element_type=jnp.float32)
    ).astype(jnp.bfloat16)
    key_all, value_all = (
        lax.all_gather(key_local, "gx", axis=0, tiled=True),
        lax.all_gather(value_local, "gx", axis=0, tiled=True),
    )
    length = key_all.shape[0]
    key_rows = key_all.reshape(length, KVH, HD)
    value_rows = value_all.reshape(length, KVH, HD)
    query_places = first_pos + jnp.arange(tokens, dtype=jnp.int32)
    key_places = jnp.arange(length, dtype=jnp.int32)
    causal = (key_places[None, :] <= query_places[:, None]) | (key_places[None, :] < span_offset[0])
    scores = (
        jnp.einsum("tkgd,skd->kgts", query, key_rows, preferred_element_type=jnp.float32) * scale
    )
    scores = jnp.where(causal, scores, -1e30)
    row_max = jnp.max(scores, axis=-1, keepdims=True)
    weights = jnp.exp(scores - row_max)
    probs = (weights / jnp.sum(weights, axis=-1, keepdims=True)).astype(jnp.bfloat16)
    attended = jnp.einsum(
        "kgts,skd->tkgd", probs, value_rows, preferred_element_type=jnp.float32
    ).astype(jnp.bfloat16)
    grad_four = out_grad[0].reshape(tokens, KVH, groups, HD)
    inner_prod = jnp.sum(grad_four.astype(jnp.float32) * attended.astype(jnp.float32), axis=-1)
    dprob = jnp.einsum("tkgd,skd->kgts", grad_four, value_rows, preferred_element_type=jnp.float32)
    dscore = (
        probs.astype(jnp.float32) * (dprob - jnp.transpose(inner_prod, (1, 2, 0))[..., None])
    ).astype(jnp.bfloat16)
    dquery = (
        jnp.einsum("kgts,skd->tkgd", dscore, key_rows, preferred_element_type=jnp.float32) * scale
    )
    query_grad = (
        rotate(dquery, cosine, sine_table, -1.0).reshape(tokens, HEADS * HD).astype(jnp.bfloat16)
    )
    block = probs
    term = jnp.einsum("kgts,tkgd->skd", block, grad_four, preferred_element_type=jnp.float32)
    value_grad = sent_and_summed(
        term.reshape(tokens * lax.axis_size("gx"), KVH * HD), "gx", 0
    ).astype(jnp.bfloat16)
    part_bq = jnp.einsum("tr,tc->rc", low_query, query_grad, preferred_element_type=jnp.float32)
    part_bv = jnp.einsum("tr,tc->rc", low_value, value_grad, preferred_element_type=jnp.float32)
    dlow_query = jnp.einsum(
        "tc,rc->tr", query_grad, b_query, preferred_element_type=jnp.float32
    ).astype(jnp.bfloat16)
    dlow_value = jnp.einsum(
        "tc,rc->tr", value_grad, b_value, preferred_element_type=jnp.float32
    ).astype(jnp.bfloat16)
    part_aq = jnp.einsum("td,tr->dr", normal, dlow_query, preferred_element_type=jnp.float32)
    part_av = jnp.einsum("td,tr->dr", normal, dlow_value, preferred_element_type=jnp.float32)
    grad_aq, grad_bq, grad_av, grad_bv = lax.psum(
        (part_aq, part_bq, part_av, part_bv), ("gx", "gy")
    )
    attn_out = attended.reshape(1, tokens, HEADS * HD)
    return (attn_out, grad_aq, grad_bq, grad_av, grad_bv)


def solution(mesh):
    return jax.shard_map(
        on_device,
        mesh=mesh,
        in_specs=(
            P(None, None, "gx"),
            P("gy", None, "gx"),
            P("gx", "gy"),
            P("gx", "gy"),
            P("gy", "gx"),
            P("gx", None),
            P("gy", "gx", None),
            P(),
            P(None, "gy"),
            P(None, "gy"),
            P(None, "gy"),
            P(),
            P(),
            P(),
            P(),
            P("gy", "gx"),
            P("gy"),
            P("gy", "gx", None),
        ),
        out_specs=(P("gy", "gx", None), P(), P(), P(), P()),
        check_vma=False,
    )
```

profile of v0, /device:TPU:1, one launch (start us, length us, event | category | flops | bytes accessed | tf_op | source)
XLA Modules:
  0.0 656.2 jit_solution(4535558930171179902)
XLA Ops:
  7.2 3.4 fusion.59
  13.9 5.3 copy.44
  19.2 52.4 %all_to_all.31 = f32[16,8,7392]{2,1,0:T(8,128)} all-to-all(f32[16,8,7392]{2,1,0:T(8,128)} %bitcast.99), channel_id=1, replica_groups=mesh['gx'=16,'gy'=8] {'gx'}, dimensions={0} | all-to-all | bytes 7569408 | tf_op jit(solution)/shard_map/all_to_all | solution.py:22
  74.0 21.7 %all_gather.12 = bf16[128,3696]{1,0:T(8,128)(2,1)S(1)} all-gather(bf16[8,3696]{1,0:T(8,128)(2,1)S(1)} %fusion.37), channel_id=1, replica_groups=mesh['gx'=16,'gy'=8] {'gx'}, dimensions={0}, use_global_device_ids=true | all-gather | bytes 1005312 | tf_op jit(solution)/shard_map/all_gather | solution.py:78
  98.5 15.4 %all_to_all.32 = f32[8,16,512]{2,1,0:T(8,128)S(1)} all-to-all(f32[8,16,512]{2,1,0:T(8,128)S(1)} %bitcast.105), channel_id=1, replica_groups=mesh['gx'=16,'gy'=8] {'gy'}, dimensions={0} | all-to-all | bytes 524288 | tf_op jit(solution)/shard_map/all_to_all | solution.py:22
  116.7 52.2 %all-reduce.5 = bf16[16,3584]{1,0:T(8,128)(2,1)S(1)} all-reduce(f32[16,3584]{1,0:T(8,128)S(1)} %fusion.46), channel_id=1, replica_groups=mesh['gx'=16,'gy'=8] {'gx'}, use_global_device_ids=true, to_apply=%region_2.3 | all-reduce | flops 57344 | bytes 344064 | tf_op jit(solution)/shard_map/psum | solution.py:85
  171.1 128.6 %all-gather.4.cloned.1.call-done = bf16[1536,3584]{1,0:T(8,128)(2,1)} async-done(((bf16[192,3584]{1,0:T(8,128)(2,1)}), bf16[1536,3584]{1,0:T(8,128)(2,1)}) %all-gather.4.cloned.1.call-update) | async-done | bytes 11010064 | tf_op jit(solution)/shard_map/all_gather | solution.py:100
  299.7 7.2 %fusion.62 = f32[1536,224]{0,1:T(8,128)S(1)} fusion(bf16[1536,3584]{1,0:T(8,128)(2,1)} %all-gather.4.cloned.1.call-done, bf16[3584,224]{0,1:T(8,128)(2,1)S(1)} %copy-done), kind=kOutput, calls=%fused_computation.82 | convolution fusion | flops 2466250752 | bytes 13991936 | tf_op jit(solution)/shard_map/dot_general | solution.py:103
  307.0 3.3 fusion.63
  310.3 3.3 fusion.64
  315.8 3.9 copy.45
  319.7 4.4 all-to-all-start.2
  324.8 29.3 %all-to-all-done.2 = f32[8,192,288]{1,2,0:T(8,128)} async-done(((f32[8,192,288]{1,2,0:T(8,128)}), f32[8,192,288]{1,2,0:T(8,128)}, u32[]{:S(2)}, u32[]{:S(2)}) %all-to-all-start.2) | async-done | bytes 1769504 | tf_op jit(solution)/shard_map/all_to_all | solution.py:109
  375.3 13.8 %all-gather.8.cloned.1.call-done = bf16[3072,256]{1,0:T(8,128)(2,1)} async-done(((bf16[192,256]{1,0:T(8,128)(2,1)}), bf16[3072,256]{1,0:T(8,128)(2,1)}) %all-gather.8.cloned.1.call-update) | async-done | bytes 1572880 | tf_op jit(solution)/shard_map/all_gather | solution.py:131
  390.8 19.7 %fusion.58 = (f32[2,7,192]{2,1,0:T(8,128)S(1)}, f32[2,7,192,3072]{3,2,1,0:T(8,128)}) fusion(bf16[3072,2,128,1]{0,2,3,1:T(8,128)(2,1)S(1)} %bitcast.103, pred[192,3072]{1,0:T(8,128)(4,1)} %fusion.14, bf16[192,2,7,64]{3,0,2,1:T(8,128)(2,1)} %get-tuple-element.10, bf16[192,2,7,64]{3,0,2,1:T(8,128)(2,1)} %get-tuple-element.9), kind=kOutput, calls=%fused_computation.78 | convolution fusion | flops 2148338688 | bytes 35891712 | tf_op jit(solution)/shard_map/sub | solution.py:145
  410.5 13.3 %divide_convert_fusion = bf16[2,7,192,3072]{3,2,1,0:T(8,128)(2,1)S(1)} fusion(f32[2,7,192,3072]{3,2,1,0:T(8,128)} %get-tuple-element.25, f32[2,7,192]{2,1,0:T(8,128)S(1)} %get-tuple-element.24), kind=kLoop, calls=%fused_computation.5 | loop fusion | flops 16515072 | bytes 49555968 | tf_op jit(solution)/shard_map/convert_element_type | solution.py:146
  423.9 8.7 %convolution_bitcast_fusion = f32[3072,2,128]{2,0,1:T(8,128)} fusion(bf16[2,7,192,3072]{3,2,1,0:T(8,128)(2,1)S(1)} %divide_convert_fusion, bf16[192,2,7,128]{3,2,1,0:T(8,128)(2,1)S(1)} %copy-done.6), kind=kOutput, calls=%fused_computation.16 | convolution fusion | flops 2113929216 | bytes 20348928 | tf_op jit(solution)/shard_map/kgts,tkgd->skd/dot_general | solution.py:163
  432.5 7.1 %copy.63 = f32[3072,2,128]{2,1,0:T(2,128)} copy(f32[3072,2,128]{2,0,1:T(8,128)} %convolution_bitcast_fusion) | data formatting | bytes 6291456 | tf_op jit(solution)/shard_map/kgts,tkgd->skd/transpose | solution.py:163
  439.7 5.5 reshape_reshape.7
  445.1 4.4 all-to-all-start.3
  452.3 9.7 %multiply_reduce_fusion.1 = (f32[192,2,7]{0,2,1:T(8,128)S(1)}, bf16[192,2,7,128]{3,0,2,1:T(8,128)(2,1)}) fusion(bf16[192,2,7,128]{3,2,1,0:T(8,128)(2,1)} %reshape_squeeze.3, bf16[2,7,192,3072]{3,2,1,0:T(8,128)(2,1)} %copy-done.3, bf16[3072,2,128,1]{2,1,0,3:T(2,128)(2,1)S(1)} %bitcast.101), kind=kOutput, calls=%fused_computation.31 | convolution fusion | flops 2115646848 | bytes 19474944 | tf_op jit(solution)/shard_map/kgts,skd->tkgd/dot_general | solution.py:147
  461.9 14.0 %fusion.18 = f32[192,2,7,128]{3,0,2,1:T(8,128)} fusion(bf16[3072,2,128,1]{0,2,3,1:T(8,128)(2,1)} %bitcast.104, bf16[2,7,192,3072]{3,2,1,0:T(8,128)(2,1)} %copy-done.3, f32[2,7,192]{2,1,0:T(8,128)S(1)} %bitcast.111, bf16[3072,2,128,1]{2,1,0,3:T(2,128)(2,1)S(1)} %bitcast.102, bf16[192,2,7,128]{3,2,1,0:T(8,128)(2,1)} %reshape_squeeze.3), kind=kOutput, calls=%fused_computation.25 | convolution fusion | flops 4261232640 | bytes 21735936 | tf_op jit(solution)/shard_map/kgts,skd->tkgd/dot_general | solution.py:157
  482.9 5.1 all-to-all-done.3
  495.5 149.1 %all-reduce.4.cloned.1.call-done = (f32[3584,64]{0,1:T(8,128)}, f32[64,1792]{1,0:T(8,128)}, f32[3584,64]{0,1:T(8,128)}, f32[64,256]{1,0:T(8,128)}) async-done(((f32[3584,64]{0,1:T(8,128)}, f32[64,1792]{1,0:T(8,128)}, f32[3584,64]{0,1:T(8,128)}, f32[64,256]{1,0:T(8,128)}), (f32[3584,64]{0,1:T(8,128)}, f32[64,1792]{1,0:T(8,128)}, f32[3584,64]{0,1:T(8,128)}, f32[64,256]{1,0:T(8,128)})) %all-reduce.4.cloned.1.call-update) | async-done | bytes 2359312 | tf_op jit(solution)/shard_map/psum | solution.py:177
  (119 shorter events, 60.2 us)
Async XLA Ops:
  7.2 292.5 %copy-start = (bf16[3584,224]{0,1:T(8,128)(2,1)S(1)}, bf16[3584,224]{0,1:T(8,128)(2,1)}, u32[]{:S(2)}) copy-start(bf16[3584,224]{0,1:T(8,128)(2,1)} %param.26) | copy-start | bytes 4816900
  7.2 292.5 %all-gather.4.cloned.1.call-start = ((), (), s32[]{:S(2)}) async-start(), calls=%async_computation.4 | async-start | bytes 12386304 | tf_op jit(solution)/shard_map/all_gather | solution.py:100
  7.2 3.5 copy-start.5
  95.7 18.2 %copy-start.26 = (bf16[1,16,512]{2,1,0:T(8,128)(2,1)S(1)}, bf16[1,16,512]{2,1,0:T(8,128)(2,1)}, u32[]{:S(2)}) copy-start(bf16[1,16,512]{2,1,0:T(8,128)(2,1)} %param.19) | copy-start | bytes 49156
  113.9 54.9 %copy-start.9 = (bf16[1,192,3584]{2,1,0:T(8,128)(2,1)S(1)}, bf16[1,192,3584]{2,1,0:T(8,128)(2,1)}, u32[]{:S(2)}) copy-start(bf16[1,192,3584]{2,1,0:T(8,128)(2,1)} %param.24) | copy-start | bytes 4128772
  114.0 54.9 %copy-start.28 = (s32[1,192]{1,0:T(1,128)S(1)}, s32[1,192]{1,0:T(1,128)}, u32[]{:S(2)}) copy-start(s32[1,192]{1,0:T(1,128)} %param.33) | copy-start | bytes 2308
  171.1 135.8 %copy-start.22 = (bf16[3584,32]{0,1:T(8,128)(2,1)S(1)}, bf16[3584,32]{0,1:T(8,128)(2,1)}, u32[]{:S(2)}) copy-start(bf16[3584,32]{0,1:T(8,128)(2,1)} %param.27) | copy-start | bytes 688132
  299.7 7.3 %copy-start.2 = (bf16[1536,3584]{1,0:T(8,128)(2,1)S(1)}, bf16[1536,3584]{1,0:T(8,128)(2,1)}, u32[]{:S(2)}) copy-start(bf16[1536,3584]{1,0:T(8,128)(2,1)} %all-gather.4.cloned.1.call-done) | copy-start | bytes 33030148
  319.7 34.3 %all-to-all-start.2 = ((f32[8,192,288]{1,2,0:T(8,128)}), f32[8,192,288]{1,2,0:T(8,128)}, u32[]{:S(2)}, u32[]{:S(2)}) async-start(f32[8,192,288]{1,2,0:T(8,128)} %copy.45), calls=%async_computation.2 | async-start | bytes 4718592 | tf_op jit(solution)/shard_map/all_to_all | solution.py:109
  324.1 33.4 %copy-start.13 = (bf16[1,192,1792]{2,1,0:T(8,128)(2,1)S(1)}, bf16[1,192,1792]{2,1,0:T(8,128)(2,1)}, u32[]{:S(2)}) copy-start(bf16[1,192,1792]{2,1,0:T(8,128)(2,1)} %param.35) | copy-start | bytes 2064388
  324.1 65.0 %all-gather.8.cloned.1.call-start = ((), (), s32[]{:S(2)}) async-start(), calls=%async_computation.6 | async-start | bytes 1671168 | tf_op jit(solution)/shard_map/all_gather | solution.py:131
  355.8 4.7 copy-start.4
  355.8 4.7 copy-start.15
  356.6 93.0 %all-gather.6.cloned.1.call-start = ((), (), s32[]{:S(2)}) async-start(), calls=%async_computation.5 | async-start | bytes 1671168 | tf_op jit(solution)/shard_map/all_gather | solution.py:132
  357.5 3.5 copy-start.16
  361.0 4.5 copy-start.18
  390.8 19.7 %copy-start.8 = (bf16[3072,256]{0,1:T(8,128)(2,1)}, bf16[3072,256]{0,1:T(8,128)(2,1)S(1)}, u32[]{:S(2)}) copy-start(bf16[3072,256]{0,1:T(8,128)(2,1)S(1)} %copy.50) | copy-start | bytes 4718596
  410.5 13.3 %copy-start.6 = (bf16[192,2,7,128]{3,2,1,0:T(8,128)(2,1)S(1)}, bf16[192,2,7,128]{3,2,1,0:T(8,128)(2,1)}, u32[]{:S(2)}) copy-start(bf16[192,2,7,128]{3,2,1,0:T(8,128)(2,1)} %reshape_squeeze.3) | copy-start | bytes 2064388
  423.8 8.7 %copy-start.3 = (bf16[2,7,192,3072]{3,2,1,0:T(8,128)(2,1)}, bf16[2,7,192,3072]{3,2,1,0:T(8,128)(2,1)S(1)}, u32[]{:S(2)}) copy-start(bf16[2,7,192,3072]{3,2,1,0:T(8,128)(2,1)S(1)} %divide_convert_fusion) | copy-start | bytes 49545220
  445.1 42.8 %all-to-all-start.3 = ((f32[16,192,256]{2,1,0:T(8,128)}), f32[16,192,256]{2,1,0:T(8,128)}, u32[]{:S(2)}, u32[]{:S(2)}) async-start(f32[16,192,256]{2,1,0:T(8,128)} %reshape_reshape.7), calls=%async_computation.3 | async-start | bytes 6291456 | tf_op jit(solution)/shard_map/all_to_all | solution.py:22
  449.6 194.9 %all-reduce.4.cloned.1.call-start = ((), (), s32[]{:S(2)}) async-start(), calls=%async_computation.7 | async-start | bytes 4718592 | tf_op jit(solution)/shard_map/psum | solution.py:177
  482.9 7.2 %copy-start.21 = (bf16[192,64]{0,1:T(8,128)(2,1)S(1)}, bf16[192,64]{0,1:T(8,128)(2,1)}, u32[]{:S(2)}) copy-start(bf16[192,64]{0,1:T(8,128)(2,1)} %convolution_convert_fusion.3) | copy-start | bytes 73732
  482.9 8.0 %copy-start.24 = (bf16[64,256]{1,0:T(8,128)(2,1)S(1)}, bf16[64,256]{1,0:T(8,128)(2,1)}, u32[]{:S(2)}) copy-start(bf16[64,256]{1,0:T(8,128)(2,1)} %param.32) | copy-start | bytes 98308
  644.5 4.7 copy-start.1
  (11 other events, 23.4 us)
Sparse Core Ops, SparseCore 0:
  171.2 128.4 all-gather.3
  356.8 32.2 all-gather.7
  390.8 32.8 all-gather.5
  492.5 152.0 all-reduce.3
where the time goes:
time: 666 us; the launch traced here: 656 us
  waiting for transfers between devices  326 us (49%)
  blocking collectives  142 us (21%)
  matrix products  88.2 us (13%)
  local copies, waits for them, and re-layouts  48 us (7%)
  other arithmetic  27.9 us (4%)
  between operations  15.4 us (2%)
  starting transfers between devices  9.15 us (1%)
    psum x1, waiting for transfers between devices, on_device(): lax.psum((part_aq, part_bq, part_av, part_bv), ('gx', 'gy'))  149 us
    all_gather x1, waiting for transfers between devices, on_device(): slab_rows = lax.all_gather(normal, 'gy', axis=0, tiled=True)  129 us
    all_to_all x2, blocking collectives, sent_and_summed(): parts = lax.all_to_all(cut_along(array, dim, size), axis, 0, 0, tiled=True)  67.9 us
    psum x1, blocking collectives, on_device(): bridge = lax.psum(bridge_part, 'gx').astype(jnp.bfloat16)  52.2 us
    all_to_all x1, waiting for transfers between devices, on_device(): lax.all_to_all(projected, 'gy', split_axis=0, concat_axis=1, tiled=True)  29.3 us
    all_gather x1, blocking collectives, on_device(): lax.all_gather(hidden, 'gx', axis=0, tiled=True)  21.7 us
    sub x1, matrix products, on_device(): weights = jnp.exp(scores - row_max)  19.7 us
    dot_general x1, matrix products, on_device(): jnp.einsum('kgts,skd->tkgd', dscore, key_rows, preferred_element_type=jnp...  14 us
  transfers between devices with their start and end apart: 6, of which 5 were waited for; matrix products, arithmetic and copies ran while one was open for 17% of the time, Pallas kernels for 0%

commit v1 on v0

--- a/solution.py
+++ b/solution.py
@@ -175,7 +175,7 @@
     part_aq = jnp.einsum("td,tr->dr", normal, dlow_query, preferred_element_type=jnp.float32)
     part_av = jnp.einsum("td,tr->dr", normal, dlow_value, preferred_element_type=jnp.float32)
     grad_aq, grad_bq, grad_av, grad_bv = lax.psum(
-        (part_aq, part_bq, part_av, part_bv), ("gx", "gy")
+        lax.psum((part_aq, part_bq, part_av, part_bv), "gx"), "gy"
     )
     attn_out = attended.reshape(1, tokens, HEADS * HD)
     return (attn_out, grad_aq, grad_bq, grad_av, grad_bv)

time: 666 us -> 759 us (1.14)
  waiting for transfers between devices: 326 us -> 421 us
    psum x1 -> x2, waiting for transfers between devices: 149 us -> 244 us  [the longest x1 125 us: on_device(): lax.psum((part_aq, part_bq, part_av, part_bv), 'gx')]
  transfers between devices with their start and end apart: 6 -> 7, of which waited for: 5 -> 6; matrix products, arithmetic and copies ran while one was open for 17% -> 15% of each run, Pallas kernels for 0% -> 0%
where the time goes in v1:
time: 759 us; the launch traced here: 750 us
  waiting for transfers between devices  421 us (55%)
  blocking collectives  142 us (19%)
  matrix products  87.9 us (12%)
  local copies, waits for them, and re-layouts  47 us (6%)
  other arithmetic  27.9 us (4%)
  between operations  15.3 us (2%)
  starting transfers between devices  9.19 us (1%)
    all_gather x1, waiting for transfers between devices, on_device(): slab_rows = lax.all_gather(normal, 'gy', axis=0, tiled=True)  129 us
    psum x1, waiting for transfers between devices, on_device(): lax.psum((part_aq, part_bq, part_av, part_bv), 'gx')  125 us
    psum x1, waiting for transfers between devices, on_device(): lax.psum(lax.psum((part_aq, part_bq, part_av, part_bv), 'gx'), 'gy')  118 us
    all_to_all x2, blocking collectives, sent_and_summed(): parts = lax.all_to_all(cut_along(array, dim, size), axis, 0, 0, tiled=True)  67.9 us
    psum x1, blocking collectives, on_device(): bridge = lax.psum(bridge_part, 'gx').astype(jnp.bfloat16)  52.2 us
    all_to_all x1, waiting for transfers between devices, on_device(): lax.all_to_all(projected, 'gy', split_axis=0, concat_axis=1, tiled=True)  29.3 us
    all_gather x1, blocking collectives, on_device(): lax.all_gather(hidden, 'gx', axis=0, tiled=True)  21.7 us
    sub x1, matrix products, on_device(): weights = jnp.exp(scores - row_max)  19.7 us
  transfers between devices with their start and end apart: 7, of which 6 were waited for; matrix products, arithmetic and copies ran while one was open for 15% of the time, Pallas kernels for 0%

profile of v1, /device:TPU:1, one launch (start us, length us, event | category | flops | bytes accessed | tf_op | source)
XLA Modules:
  0.0 749.7 jit_solution(3756903414158784054)
XLA Ops:
  7.2 3.4 fusion.59
  13.9 5.3 copy.44
  19.2 52.4 %all_to_all.31 = f32[16,8,7392]{2,1,0:T(8,128)} all-to-all(f32[16,8,7392]{2,1,0:T(8,128)} %bitcast.99), channel_id=1, replica_groups=mesh['gx'=16,'gy'=8] {'gx'}, dimensions={0} | all-to-all | bytes 7569408 | tf_op jit(solution)/shard_map/all_to_all | solution.py:22
  74.0 21.7 %all_gather.12 = bf16[128,3696]{1,0:T(8,128)(2,1)S(1)} all-gather(bf16[8,3696]{1,0:T(8,128)(2,1)S(1)} %fusion.37), channel_id=1, replica_groups=mesh['gx'=16,'gy'=8] {'gx'}, dimensions={0}, use_global_device_ids=true | all-gather | bytes 1005312 | tf_op jit(solution)/shard_map/all_gather | solution.py:78
  98.5 15.4 %all_to_all.32 = f32[8,16,512]{2,1,0:T(8,128)S(1)} all-to-all(f32[8,16,512]{2,1,0:T(8,128)S(1)} %bitcast.105), channel_id=1, replica_groups=mesh['gx'=16,'gy'=8] {'gy'}, dimensions={0} | all-to-all | bytes 524288 | tf_op jit(solution)/shard_map/all_to_all | solution.py:22
  116.7 52.2 %all-reduce.9 = bf16[16,3584]{1,0:T(8,128)(2,1)S(1)} all-reduce(f32[16,3584]{1,0:T(8,128)S(1)} %fusion.46), channel_id=1, replica_groups=mesh['gx'=16,'gy'=8] {'gx'}, use_global_device_ids=true, to_apply=%region_2.3 | all-reduce | flops 57344 | bytes 344064 | tf_op jit(solution)/shard_map/psum | solution.py:85
  171.1 128.6 %all-gather.4.cloned.1.call-done = bf16[1536,3584]{1,0:T(8,128)(2,1)} async-done(((bf16[192,3584]{1,0:T(8,128)(2,1)}), bf16[1536,3584]{1,0:T(8,128)(2,1)}) %all-gather.4.cloned.1.call-update) | async-done | bytes 11010064 | tf_op jit(solution)/shard_map/all_gather | solution.py:100
  299.7 7.2 fusion.62
  310.3 3.3 fusion.64
  315.8 3.9 copy.45
  319.7 4.4 all-to-all-start.2
  324.8 29.3 %all-to-all-done.2 = f32[8,192,288]{1,2,0:T(8,128)} async-done(((f32[8,192,288]{1,2,0:T(8,128)}), f32[8,192,288]{1,2,0:T(8,128)}, u32[]{:S(2)}, u32[]{:S(2)}) %all-to-all-start.2) | async-done | bytes 1769504 | tf_op jit(solution)/shard_map/all_to_all | solution.py:109
  375.3 13.8 %all-gather.8.cloned.1.call-done = bf16[3072,256]{1,0:T(8,128)(2,1)} async-done(((bf16[192,256]{1,0:T(8,128)(2,1)}), bf16[3072,256]{1,0:T(8,128)(2,1)}) %all-gather.8.cloned.1.call-update) | async-done | bytes 1572880 | tf_op jit(solution)/shard_map/all_gather | solution.py:131
  390.8 19.7 %fusion.58 = (f32[2,7,192]{2,1,0:T(8,128)S(1)}, f32[2,7,192,3072]{3,2,1,0:T(8,128)}) fusion(bf16[3072,2,128,1]{0,2,3,1:T(8,128)(2,1)S(1)} %bitcast.103, pred[192,3072]{1,0:T(8,128)(4,1)} %fusion.14, bf16[192,2,7,64]{3,0,2,1:T(8,128)(2,1)} %get-tuple-element.14, bf16[192,2,7,64]{3,0,2,1:T(8,128)(2,1)} %get-tuple-element.13), kind=kOutput, calls=%fused_computation.78 | convolution fusion | flops 2148338688 | bytes 35891712 | tf_op jit(solution)/shard_map/sub | solution.py:145
  410.5 13.3 %divide_convert_fusion = bf16[2,7,192,3072]{3,2,1,0:T(8,128)(2,1)S(1)} fusion(f32[2,7,192,3072]{3,2,1,0:T(8,128)} %get-tuple-element.29, f32[2,7,192]{2,1,0:T(8,128)S(1)} %get-tuple-element.28), kind=kLoop, calls=%fused_computation.5 | loop fusion | flops 16515072 | bytes 49555968 | tf_op jit(solution)/shard_map/convert_element_type | solution.py:146
  423.9 8.7 %convolution_bitcast_fusion = f32[3072,2,128]{2,0,1:T(8,128)} fusion(bf16[2,7,192,3072]{3,2,1,0:T(8,128)(2,1)S(1)} %divide_convert_fusion, bf16[192,2,7,128]{3,2,1,0:T(8,128)(2,1)S(1)} %copy-done.6), kind=kOutput, calls=%fused_computation.16 | convolution fusion | flops 2113929216 | bytes 20348928 | tf_op jit(solution)/shard_map/kgts,tkgd->skd/dot_general | solution.py:163
  432.5 7.1 copy.63
  439.7 5.5 reshape_reshape.7
  445.1 4.5 all-to-all-start.3
  452.3 9.7 %multiply_reduce_fusion.1 = (f32[192,2,7]{0,2,1:T(8,128)S(1)}, bf16[192,2,7,128]{3,0,2,1:T(8,128)(2,1)}) fusion(bf16[192,2,7,128]{3,2,1,0:T(8,128)(2,1)} %reshape_squeeze.3, bf16[2,7,192,3072]{3,2,1,0:T(8,128)(2,1)} %copy-done.3, bf16[3072,2,128,1]{2,1,0,3:T(2,128)(2,1)S(1)} %bitcast.101), kind=kOutput, calls=%fused_computation.31 | convolution fusion | flops 2115646848 | bytes 19474944 | tf_op jit(solution)/shard_map/kgts,skd->tkgd/dot_general | solution.py:147
  462.0 13.8 %fusion.18 = f32[192,2,7,128]{3,0,2,1:T(8,128)} fusion(bf16[3072,2,128,1]{0,2,3,1:T(8,128)(2,1)} %bitcast.104, bf16[2,7,192,3072]{3,2,1,0:T(8,128)(2,1)} %copy-done.3, f32[2,7,192]{2,1,0:T(8,128)S(1)} %bitcast.111, bf16[3072,2,128,1]{2,1,0,3:T(2,128)(2,1)S(1)} %bitcast.102, bf16[192,2,7,128]{3,2,1,0:T(8,128)(2,1)} %reshape_squeeze.3), kind=kOutput, calls=%fused_computation.25 | convolution fusion | flops 4261232640 | bytes 21735936 | tf_op jit(solution)/shard_map/kgts,skd->tkgd/dot_general | solution.py:157
  482.6 5.4 all-to-all-done.3
  492.4 125.4 %all-reduce.6.cloned.1.call-done = (f32[3584,64]{0,1:T(8,128)}, f32[64,1792]{1,0:T(8,128)}, f32[3584,64]{0,1:T(8,128)}, f32[64,256]{1,0:T(8,128)}) async-done(((f32[3584,64]{0,1:T(8,128)}, f32[64,1792]{1,0:T(8,128)}, f32[3584,64]{0,1:T(8,128)}, f32[64,256]{1,0:T(8,128)}), (f32[3584,64]{0,1:T(8,128)}, f32[64,1792]{1,0:T(8,128)}, f32[3584,64]{0,1:T(8,128)}, f32[64,256]{1,0:T(8,128)})) %all-reduce.6.cloned.1.call-update) | async-done | bytes 2359312 | tf_op jit(solution)/shard_map/psum | solution.py:178
  619.9 118.2 %all-reduce.8.cloned.1.call-done = (f32[3584,64]{0,1:T(8,128)}, f32[64,1792]{1,0:T(8,128)}, f32[3584,64]{0,1:T(8,128)}, f32[64,256]{1,0:T(8,128)}) async-done(((f32[3584,64]{0,1:T(8,128)}, f32[64,1792]{1,0:T(8,128)}, f32[3584,64]{0,1:T(8,128)}, f32[64,256]{1,0:T(8,128)}), (f32[3584,64]{0,1:T(8,128)}, f32[64,1792]{1,0:T(8,128)}, f32[3584,64]{0,1:T(8,128)}, f32[64,256]{1,0:T(8,128)})) %all-reduce.8.cloned.1.call-update) | async-done | bytes 2359312 | tf_op jit(solution)/shard_map/psum | solution.py:177
  (122 shorter events, 62.4 us)
Async XLA Ops:
  7.2 292.5 %copy-start = (bf16[3584,224]{0,1:T(8,128)(2,1)S(1)}, bf16[3584,224]{0,1:T(8,128)(2,1)}, u32[]{:S(2)}) copy-start(bf16[3584,224]{0,1:T(8,128)(2,1)} %param.26) | copy-start | bytes 4816900
  7.2 292.5 %all-gather.4.cloned.1.call-start = ((), (), s32[]{:S(2)}) async-start(), calls=%async_computation.4 | async-start | bytes 12386304 | tf_op jit(solution)/shard_map/all_gather | solution.py:100
  95.7 18.2 %copy-start.26 = (bf16[1,16,512]{2,1,0:T(8,128)(2,1)S(1)}, bf16[1,16,512]{2,1,0:T(8,128)(2,1)}, u32[]{:S(2)}) copy-start(bf16[1,16,512]{2,1,0:T(8,128)(2,1)} %param.19) | copy-start | bytes 49156
  113.9 54.9 %copy-start.9 = (bf16[1,192,3584]{2,1,0:T(8,128)(2,1)S(1)}, bf16[1,192,3584]{2,1,0:T(8,128)(2,1)}, u32[]{:S(2)}) copy-start(bf16[1,192,3584]{2,1,0:T(8,128)(2,1)} %param.24) | copy-start | bytes 4128772
  113.9 54.9 %copy-start.28 = (s32[1,192]{1,0:T(1,128)S(1)}, s32[1,192]{1,0:T(1,128)}, u32[]{:S(2)}) copy-start(s32[1,192]{1,0:T(1,128)} %param.33) | copy-start | bytes 2308
  171.1 135.8 %copy-start.22 = (bf16[3584,32]{0,1:T(8,128)(2,1)S(1)}, bf16[3584,32]{0,1:T(8,128)(2,1)}, u32[]{:S(2)}) copy-start(bf16[3584,32]{0,1:T(8,128)(2,1)} %param.27) | copy-start | bytes 688132
  299.7 7.3 copy-start.2
  319.7 34.3 %all-to-all-start.2 = ((f32[8,192,288]{1,2,0:T(8,128)}), f32[8,192,288]{1,2,0:T(8,128)}, u32[]{:S(2)}, u32[]{:S(2)}) async-start(f32[8,192,288]{1,2,0:T(8,128)} %copy.45), calls=%async_computation.2 | async-start | bytes 4718592 | tf_op jit(solution)/shard_map/all_to_all | solution.py:109
  324.1 33.4 %copy-start.13 = (bf16[1,192,1792]{2,1,0:T(8,128)(2,1)S(1)}, bf16[1,192,1792]{2,1,0:T(8,128)(2,1)}, u32[]{:S(2)}) copy-start(bf16[1,192,1792]{2,1,0:T(8,128)(2,1)} %param.35) | copy-start | bytes 2064388
  324.1 65.0 %all-gather.8.cloned.1.call-start = ((), (), s32[]{:S(2)}) async-start(), calls=%async_computation.6 | async-start | bytes 1671168 | tf_op jit(solution)/shard_map/all_gather | solution.py:131
  355.8 4.7 copy-start.4
  355.8 4.7 copy-start.15
  356.6 93.0 %all-gather.6.cloned.1.call-start = ((), (), s32[]{:S(2)}) async-start(), calls=%async_computation.5 | async-start | bytes 1671168 | tf_op jit(solution)/shard_map/all_gather | solution.py:132
  361.0 4.5 copy-start.18
  390.8 19.7 %copy-start.8 = (bf16[3072,256]{0,1:T(8,128)(2,1)}, bf16[3072,256]{0,1:T(8,128)(2,1)S(1)}, u32[]{:S(2)}) copy-start(bf16[3072,256]{0,1:T(8,128)(2,1)S(1)} %copy.50) | copy-start | bytes 4718596
  410.5 13.3 %copy-start.6 = (bf16[192,2,7,128]{3,2,1,0:T(8,128)(2,1)S(1)}, bf16[192,2,7,128]{3,2,1,0:T(8,128)(2,1)}, u32[]{:S(2)}) copy-start(bf16[192,2,7,128]{3,2,1,0:T(8,128)(2,1)} %reshape_squeeze.3) | copy-start | bytes 2064388
  423.8 8.7 %copy-start.3 = (bf16[2,7,192,3072]{3,2,1,0:T(8,128)(2,1)}, bf16[2,7,192,3072]{3,2,1,0:T(8,128)(2,1)S(1)}, u32[]{:S(2)}) copy-start(bf16[2,7,192,3072]{3,2,1,0:T(8,128)(2,1)S(1)} %divide_convert_fusion) | copy-start | bytes 49545220
  445.1 42.8 %all-to-all-start.3 = ((f32[16,192,256]{2,1,0:T(8,128)}), f32[16,192,256]{2,1,0:T(8,128)}, u32[]{:S(2)}, u32[]{:S(2)}) async-start(f32[16,192,256]{2,1,0:T(8,128)} %reshape_reshape.7), calls=%async_computation.3 | async-start | bytes 6291456 | tf_op jit(solution)/shard_map/all_to_all | solution.py:22
  449.6 168.2 %all-reduce.6.cloned.1.call-start = ((), (), s32[]{:S(2)}) async-start(), calls=%async_computation.7 | async-start | bytes 4718592 | tf_op jit(solution)/shard_map/psum | solution.py:178
  482.6 7.5 copy-start.21
  482.6 8.3 %copy-start.24 = (bf16[64,256]{1,0:T(8,128)(2,1)S(1)}, bf16[64,256]{1,0:T(8,128)(2,1)}, u32[]{:S(2)}) copy-start(bf16[64,256]{1,0:T(8,128)(2,1)} %param.32) | copy-start | bytes 98308
  492.4 125.5 %copy-start.7 = (bf16[192,2,7,128]{3,0,2,1:T(8,128)(2,1)S(1)}, bf16[192,2,7,128]{3,0,2,1:T(8,128)(2,1)}, u32[]{:S(2)}) copy-start(bf16[192,2,7,128]{3,0,2,1:T(8,128)(2,1)} %get-tuple-element.31) | copy-start | bytes 2064388
  492.4 245.7 %all-reduce.8.cloned.1.call-start = ((), (), s32[]{:S(2)}) async-start(), calls=%async_computation.8 | async-start | bytes 4718592 | tf_op jit(solution)/shard_map/psum | solution.py:177
  738.1 4.7 copy-start.1
  (12 other events, 29.3 us)
Sparse Core Ops, SparseCore 0:
  171.2 128.4 all-gather.3
  356.8 32.2 all-gather.7
  390.8 32.8 all-gather.5
  492.5 125.3 all-reduce.5
  620.5 117.5 all-reduce.7
